TPU v7x, 512 devices: a whole 4x4x16 slice. The times are simulated.
512 devices in a mesh: row: 16 (over z_hi, y), col: 4 (over x), cuts: 8 (over z_lo, core).
Axes of the slice: x: 4, y: 4, z: 16 (z_hi: 4, z_lo: 4; z = z_hi * 4 + z_lo), core: 2. Of those that a mesh axis runs over, the one named last changes fastest.
Arguments:
- warm: float32 [40, 131072], P('cuts', ('row', 'col')), may hold values from -6 to 6
- tiles: float32 [22016, 128, 128], P(('row', 'col', 'cuts')), may hold values from -0.125 to 0.125
- tile_rows: int32 [22016], P(('row', 'col', 'cuts')), may hold values from -1 to 1023, as said below
- tile_cols: int32 [22016], P(('row', 'col', 'cuts')), may hold values from 0 to 1023, as said below
Outputs:
- basis: float32 [40, 131072], P('cuts', ('row', 'col'))
- residual: float32 [40, 131072], P('cuts', ('row', 'col'))
Inputs may be any that keep to these rules, and one draw needn't show every extreme that they name: `tile_rows`: slots come in groups of 344; group r * (size of col) + c belongs to the grid position with row index r and column index c. A group's tiles lie in the block rows r * (size of col) * 16 up to (r + 1) * (size of col) * 16 - 1, and in block columns j with (j // 16) % (size of col) = c. No block appears twice. In each group the live slots come first and fill at least half of it; some group is full. Block rows hold uneven numbers of tiles. `tile_cols`: see tile_rows; an empty slot's column is that of some block the group may hold.
All inputs are finite; a program needn't handle non-finite values.
Results may differ from a plain program's by a relative error of at most 0.0003.
Values sent between devices are 32-bit elements; how exact they have to be, the bound alone decides.
A program may use at most 64 MiB of HBM per device.

v0:
```python
import jax
import jax.numpy as jnp
from jax import lax
from jax.sharding import PartitionSpec as P


def copy_for_each(shard, axis):
    devices = lax.axis_size(axis)
    return lax.all_to_all(
        jnp.broadcast_to(shard[None], (devices, *shard.shape)), axis, 0, 0, tiled=True
    )


def in_order(parts, dim):
    dims = list(parts.shape[1:])
    dims[dim] *= parts.shape[0]
    return jnp.moveaxis(parts, 0, dim).reshape(dims)


def collect(shard, axis, dim):
    parts = copy_for_each(shard, axis)
    return in_order(parts, dim)


def in_blocks(shard, dim, devices):
    dims = shard.shape
    parts = shard.reshape(*dims[:dim], devices, dims[dim] // devices, *dims[dim + 1 :])
    return jnp.moveaxis(parts, dim, 0)


def summed_on_arrival(shard, axis, dim):
    parts = in_blocks(shard, dim, lax.axis_size(axis))
    arrived = lax.all_to_all(parts, axis, split_axis=0, concat_axis=0, tiled=True)
    return arrived.sum(axis=0)


def over_copies(shard, axis):
    everything = copy_for_each(shard, axis)
    return jnp.sum(everything, axis=0)


def block_product(panel, tiles, rows, positions, base, out_blocks):
    count_rows = panel.shape[0]
    block = tiles.shape[1]
    blocks = panel.reshape(count_rows, -1, block)
    picked = jnp.take(blocks, positions, axis=1)
    prods = jnp.einsum("suv,ksv->ksu", tiles, picked, precision=lax.Precision.HIGHEST)
    local = rows - base
    onehot = (local[:, None] == jnp.arange(out_blocks, dtype=jnp.int32)[None, :]).astype(
        jnp.float32
    )
    summed = jnp.einsum("ksu,sb->kbu", prods, onehot, precision=lax.Precision.HIGHEST)
    return summed.reshape(count_rows, out_blocks * block)


def operator_apply(vectors, tiles, rows, positions, base, out_blocks):
    panel = collect(vectors, "cuts", 0)
    panel = lax.all_gather(panel, "row", axis=1, tiled=True)
    partial_value = block_product(panel, tiles, rows, positions, base, out_blocks)
    partial_value = summed_on_arrival(partial_value, "col", 1)
    return summed_on_arrival(partial_value, "cuts", 0)


def shards(warm, tiles, tile_rows, tile_cols):
    ncol = lax.axis_size("col")
    nrow = lax.axis_size("row")
    block = tiles.shape[1]
    seg_blocks = warm.shape[1] // block
    out_blocks = ncol * seg_blocks
    items = warm.shape[1] * nrow * ncol
    base = lax.axis_index("row") * out_blocks
    segment = tile_cols // seg_blocks
    positions = segment // ncol * seg_blocks + tile_cols % seg_blocks
    image = operator_apply(warm, tiles, tile_rows, positions, base, out_blocks)
    whole = collect(image, "cuts", 0)
    local_gram = jnp.dot(
        whole, whole.T, precision=lax.Precision.HIGHEST, preferred_element_type=jnp.float32
    )
    gram = over_copies(local_gram, ("row", "col")) / items
    lower = jnp.linalg.cholesky(gram)
    kloc = warm.shape[0]
    start = lax.axis_index("cuts") * kloc
    inverse = lax.linalg.triangular_solve(
        lower, jnp.eye(whole.shape[0], dtype=jnp.float32), left_side=True, lower=True
    )
    mine_rows = lax.dynamic_slice_in_dim(inverse, start, kloc, 0)
    basis = jnp.dot(
        mine_rows, whole, precision=lax.Precision.HIGHEST, preferred_element_type=jnp.float32
    )
    basis_all = collect(basis, "cuts", 0)
    product = operator_apply(basis, tiles, tile_rows, positions, base, out_blocks)
    local_projection = jnp.dot(
        basis_all, product.T, precision=lax.Precision.HIGHEST, preferred_element_type=jnp.float32
    )
    projected = over_copies(local_projection, ("row", "col")) / items
    residual = product - jnp.dot(
        projected.T, basis_all, precision=lax.Precision.HIGHEST, preferred_element_type=jnp.float32
    )
    return (basis, residual)


def solution(mesh):
    return jax.shard_map(
        shards,
        mesh=mesh,
        in_specs=(
            P("cuts", ("row", "col")),
            P(("row", "col", "cuts"), None, None),
            P(("row", "col", "cuts")),
            P(("row", "col", "cuts")),
        ),
        out_specs=(P("cuts", ("row", "col")), P("cuts", ("row", "col"))),
        check_vma=False,
    )
```

profile of v0, /device:TPU:1, one launch (start us, length us, event | category | flops | bytes accessed | tf_op | source)
XLA Modules:
  0.0 604.3 jit_solution(9353652540865754813)
XLA Ops:
  7.2 0.0 copy-start
  7.2 0.0 copy-start.3
  7.2 0.0 all-gather.3.cloned.1.call-start
  7.2 1.0 broadcast_in_dim.20
  8.3 23.5 %all_to_all.46 = f32[8,5,2048]{2,1,0:T(8,128)S(1)} all-to-all(f32[8,5,2048]{2,1,0:T(8,128)S(1)} %broadcast_in_dim.20), channel_id=1, replica_groups=mesh['row'=16,'col'=4,'cuts'=8] {'cuts'}, dimensions={0} | all-to-all | bytes 655360 | tf_op jit(solution)/shard_map/all_to_all | solution.py:9
  31.8 0.8 reshape.46
  32.6 0.0 all-gather.3.cloned.1.call-update
  32.7 0.0 copy-done.4
  32.7 155.9 %all-gather.3.cloned.1.call-done = f32[40,32768]{1,0:T(8,128)} async-done(((f32[40,2048]{1,0:T(8,128)}), f32[40,32768]{1,0:T(8,128)}) %all-gather.3.cloned.1.call-update) | async-done | bytes 5242896 | tf_op jit(solution)/shard_map/all_gather | solution.py:58
  188.6 5.2 copy_bitcast_fusion.1
  193.8 4.0 gather_fusion
  197.8 6.9 %convolution_bitcast_fusion.3 = f32[40,43,128]{2,0,1:T(8,128)S(1)} fusion(f32[43,128,128]{2,1,0:T(8,128)S(1)} %copy-done, f32[43,40,128]{2,1,0:T(8,128)} %gather_fusion, pred[43]{0:T(512)(128)(4,1)S(1)} %get-tuple-element.3), kind=kOutput, calls=%fused_computation.8 | convolution fusion | flops 338385920 | bytes 4579371 | tf_op jit(solution)/shard_map/suv,ksv->ksu/dot_general | solution.py:47
  204.6 1.9 convolution_bitcast_fusion.1
  206.5 2.7 reshape_reshape.6
  209.2 2.1 copy.55
  211.2 20.7 %all_to_all.47 = f32[4,40,2048]{2,1,0:T(8,128)} all-to-all(f32[4,40,2048]{2,1,0:T(8,128)S(1)} %bitcast.55), channel_id=1, replica_groups=mesh['row'=16,'col'=4,'cuts'=8] {'col'}, dimensions={0} | all-to-all | bytes 2621440 | tf_op jit(solution)/shard_map/all_to_all | solution.py:33
  232.0 2.2 reduce_sum.56
  234.1 1.0 reshape.48
  235.1 19.3 %all_to_all.48 = f32[8,5,2048]{2,1,0:T(8,128)} all-to-all(f32[8,5,2048]{2,1,0:T(8,128)S(1)} %reshape.48), channel_id=1, replica_groups=mesh['row'=16,'col'=4,'cuts'=8] {'cuts'}, dimensions={0} | all-to-all | bytes 655360 | tf_op jit(solution)/shard_map/all_to_all | solution.py:33
  254.4 1.1 reduce_sum.57
  255.6 18.4 %all_to_all.49 = f32[8,5,2048]{2,1,0:T(8,128)} all-to-all(f32[8,5,2048]{2,1,0:T(8,128)S(1)} %broadcast_in_dim.22), channel_id=1, replica_groups=mesh['row'=16,'col'=4,'cuts'=8] {'cuts'}, dimensions={0} | all-to-all | bytes 655360 | tf_op jit(solution)/shard_map/all_to_all | solution.py:9
  274.0 1.1 reshape.49
  275.1 0.4 fusion.28
  275.5 1.1 broadcast_in_dim.23
  276.6 3.2 reshape.76
  279.8 10.5 %all-to-all-start.4 = ((f32[64,1,1600]{2,1,0:T(1,128)}), f32[64,1,1600]{2,1,0:T(1,128)}, u32[]{:S(2)}, u32[]{:S(2)}) async-start(f32[64,1,1600]{2,1,0:T(1,128)} %reshape.76), calls=%async_computation.4 | async-start | bytes 851968 | tf_op jit(solution)/shard_map/all_to_all | solution.py:9
  290.3 0.2 all-gather.5.cloned.1.call-start
  290.5 24.7 %all-to-all-done.4 = f32[64,1,1600]{2,1,0:T(1,128)} async-done(((f32[64,1,1600]{2,1,0:T(1,128)}), f32[64,1,1600]{2,1,0:T(1,128)}, u32[]{:S(2)}, u32[]{:S(2)}) %all-to-all-start.4) | async-done | bytes 409632 | tf_op jit(solution)/shard_map/all_to_all | solution.py:9
  315.2 0.5 broadcast.112
  315.8 3.4 reduce.6
  319.2 2.6 reshape.77
  321.8 1.4 reduce_sum.58
  323.2 0.1 copy.39
  323.3 3.6 cholesky.17
  327.0 0.6 compare_reduce_fusion
  327.7 0.7 fusion.13
  328.3 3.1 custom-call.6
  331.4 0.2 fusion.14
  331.6 0.3 fusion.20
  331.9 0.0 copy-start.2
  331.9 22.3 %all_to_all.50 = f32[8,5,2048]{2,1,0:T(8,128)S(1)} all-to-all(f32[8,5,2048]{2,1,0:T(8,128)S(1)} %broadcast_in_dim.24), channel_id=1, replica_groups=mesh['row'=16,'col'=4,'cuts'=8] {'cuts'}, dimensions={0} | all-to-all | bytes 655360 | tf_op jit(solution)/shard_map/all_to_all | solution.py:9
  354.2 0.8 reshape.50
  355.0 0.0 all-gather.5.cloned.1.call-update
  355.0 146.8 %all-gather.5.cloned.1.call-done = f32[40,32768]{1,0:T(8,128)} async-done(((f32[40,2048]{1,0:T(8,128)}), f32[40,32768]{1,0:T(8,128)}) %all-gather.5.cloned.1.call-update) | async-done | bytes 5242896 | tf_op jit(solution)/shard_map/all_gather | solution.py:58
  501.9 5.1 copy_bitcast_fusion
  507.0 4.0 gather_fusion.1
  511.0 6.9 %convolution_bitcast_fusion.2 = f32[40,43,128]{2,0,1:T(8,128)S(1)} fusion(f32[43,128,128]{2,1,0:T(8,128)S(1)} %copy-done, f32[43,40,128]{2,1,0:T(8,128)} %gather_fusion.1, pred[43]{0:T(512)(128)(4,1)S(1)} %get-tuple-element.3), kind=kOutput, calls=%fused_computation.7 | convolution fusion | flops 338385920 | bytes 4579371 | tf_op jit(solution)/shard_map/suv,ksv->ksu/dot_general | solution.py:47
  517.9 1.9 convolution_bitcast_fusion
  519.8 2.7 reshape_reshape.7
  522.4 2.1 copy.54
  524.5 0.0 copy-start.1
  524.5 20.8 %all_to_all.51 = f32[4,40,2048]{2,1,0:T(8,128)} all-to-all(f32[4,40,2048]{2,1,0:T(8,128)S(1)} %bitcast.56), channel_id=1, replica_groups=mesh['row'=16,'col'=4,'cuts'=8] {'col'}, dimensions={0} | all-to-all | bytes 2621440 | tf_op jit(solution)/shard_map/all_to_all | solution.py:33
  545.4 1.4 reduce_sum.60
  546.8 0.8 reshape.52
  547.6 20.3 %all_to_all.52 = f32[8,5,2048]{2,1,0:T(8,128)} all-to-all(f32[8,5,2048]{2,1,0:T(8,128)} %reshape.52), channel_id=1, replica_groups=mesh['row'=16,'col'=4,'cuts'=8] {'cuts'}, dimensions={0} | all-to-all | bytes 655360 | tf_op jit(solution)/shard_map/all_to_all | solution.py:33
  568.0 1.1 reduce_sum.61
  569.1 0.3 fusion.29
  569.4 0.1 broadcast_bitcast_fusion
  569.5 0.2 reshape.78
  569.6 26.0 %all_to_all.53 = f32[64,1,200]{2,1,0:T(1,128)S(1)} all-to-all(f32[64,1,200]{2,1,0:T(1,128)S(1)} %reshape.78), channel_id=1, replica_groups=mesh['row'=16,'col'=4,'cuts'=8] {'row','col'}, dimensions={0} | all-to-all | bytes 102400 | tf_op jit(solution)/shard_map/all_to_all | solution.py:9
  595.6 0.8 reduce.7
  596.4 0.1 reshape.79
  596.5 0.1 bitcast_reduce_fusion
  596.6 0.9 convolution_subtract_fusion
  (12 shorter events, 0.2 us)
Async XLA Ops:
  7.2 190.6 %copy-start = (f32[43,128,128]{2,1,0:T(8,128)S(1)}, f32[43,128,128]{2,1,0:T(8,128)}, u32[]{:S(2)}) copy-start(f32[43,128,128]{2,1,0:T(8,128)} %param.7) | copy-start | bytes 8454148
  7.2 25.4 %copy-start.3 = (s32[43]{0:T(128)S(1)}, s32[43]{0:T(128)}, u32[]{:S(2)}) copy-start(s32[43]{0:T(128)} %param.9) | copy-start | bytes 520
  7.2 25.5 %copy-start.4 = (s32[43]{0:T(128)S(1)}, s32[43]{0:T(128)}, u32[]{:S(2)}) copy-start(s32[43]{0:T(128)} %param.8) | copy-start | bytes 520
  7.2 181.4 %all-gather.3.cloned.1.call-start = ((), (), s32[]{:S(2)}) async-start(), calls=%async_computation.9 | async-start | bytes 5570560 | tf_op jit(solution)/shard_map/all_gather | solution.py:58
  279.8 35.4 %all-to-all-start.4 = ((f32[64,1,1600]{2,1,0:T(1,128)}), f32[64,1,1600]{2,1,0:T(1,128)}, u32[]{:S(2)}, u32[]{:S(2)}) async-start(f32[64,1,1600]{2,1,0:T(1,128)} %reshape.76), calls=%async_computation.4 | async-start | bytes 851968 | tf_op jit(solution)/shard_map/all_to_all | solution.py:9
  290.3 211.6 %all-gather.5.cloned.1.call-start = ((), (), s32[]{:S(2)}) async-start(), calls=%async_computation.10 | async-start | bytes 5570560 | tf_op jit(solution)/shard_map/all_gather | solution.py:58
  331.9 175.1 %copy-start.2 = (f32[5,2048]{1,0:T(8,128)}, f32[5,2048]{1,0:T(8,128)S(1)}, u32[]{:S(2)}) copy-start(f32[5,2048]{1,0:T(8,128)S(1)} %fusion.20) | copy-start | bytes 122884
  524.5 44.5 %copy-start.1 = (f32[40,2048]{1,0:T(8,128)S(1)}, f32[40,2048]{1,0:T(8,128)}, u32[]{:S(2)}) copy-start(f32[40,2048]{1,0:T(8,128)} %reshape.50) | copy-start | bytes 983044
Sparse Core Ops, SparseCore 0:
  32.7 155.8 all-gather.2
  355.2 146.6 all-gather.4
where the time goes:
time: 606 us; the launch traced here: 604 us
  waiting for transfers between devices  327 us (54%)
  blocking collectives  171 us (28%)
  local copies, waits for them, and re-layouts  41.4 us (7%)
  other arithmetic  19.6 us (3%)
  matrix products  19.6 us (3%)
  between operations  14.3 us (2%)
  starting transfers between devices  10.7 us (2%)
    all_gather x2, waiting for transfers between devices, operator_apply(): panel = lax.all_gather(panel, 'row', axis=1, tiled=True)  303 us
    all_to_all x4, blocking collectives, copy_for_each(): lax.all_to_all(jnp.broadcast_to(shard[None], (devices, *shard.shape)), ax...  90.2 us
    all_to_all x4, blocking collectives, summed_on_arrival(): lax.all_to_all(parts, axis, split_axis=0, concat_axis=0, tiled=True)  81.2 us
    all_to_all x1, waiting for transfers between devices, copy_for_each(): lax.all_to_all(jnp.broadcast_to(shard[None], (devices, *shard.shape)), ax...  24.7 us
    dot_general x2, matrix products, block_product(): jnp.einsum('suv,ksv->ksu', tiles, picked, precision=lax.Precision.HIGHEST)  13.7 us
  transfers between devices with their start and end apart: 3, of which 3 were waited for; matrix products, arithmetic and copies ran while one was open for 0% of the time, Pallas kernels for 0%

commit v1 on v0

--- a/solution.py
+++ b/solution.py
@@ -2,6 +2,13 @@
 import jax.numpy as jnp
 from jax import lax
 from jax.sharding import PartitionSpec as P
+
+
+def gather_over(shard, mesh_axis, dim):
+    size = lax.axis_size(mesh_axis)
+    parts = jnp.stack([shard for _ in range(size)])
+    parts = lax.all_to_all(parts, mesh_axis, split_axis=0, concat_axis=0)
+    return jnp.concatenate(parts, axis=dim)
 
 
 def copy_for_each(shard, axis):
@@ -55,7 +62,7 @@
 
 def operator_apply(vectors, tiles, rows, positions, base, out_blocks):
     panel = collect(vectors, "cuts", 0)
-    panel = lax.all_gather(panel, "row", axis=1, tiled=True)
+    panel = gather_over(panel, "row", 1)
     partial_value = block_product(panel, tiles, rows, positions, base, out_blocks)
     partial_value = summed_on_arrival(partial_value, "col", 1)
     return summed_on_arrival(partial_value, "cuts", 0)

time: 606 us -> 813 us (1.34)
  blocking collectives: 171 us -> 407 us
  waiting for transfers between devices: 327 us -> 259 us
  local copies, waits for them, and re-layouts: 41.4 us -> 78.3 us
  starting transfers between devices: 10.7 us -> 26.9 us
  between operations: 14.3 us -> 0.85 us
    all_gather x2 -> x0, waiting for transfers between devices: 303 us -> none  [operator_apply(): panel = lax.all_gather(panel, 'row', axis=1, tiled=True)]
    all_to_all x0 -> x1, blocking collectives: none -> 237 us  [gather_over(): parts = lax.all_to_all(parts, mesh_axis, split_axis=0, concat_axis=0)]
    all_to_all x0 -> x1, waiting for transfers between devices: none -> 234 us  [gather_over(): parts = lax.all_to_all(parts, mesh_axis, split_axis=0, concat_axis=0)]
    another operation x0 -> x8, local copies, waits for them, and re-layouts: none -> 35.7 us  [the longest x4 29.2 us: block_product(): blocks = panel.reshape(count_rows, -1, block)]
    all_to_all x0 -> x1, starting transfers between devices: none -> 13 us  [gather_over(): parts = lax.all_to_all(parts, mesh_axis, split_axis=0, concat_axis=0)]
  transfers between devices with their start and end apart: 3 -> 2, of which waited for: 3 -> 2; matrix products, arithmetic and copies ran while one was open for 0% -> 0% of each run, Pallas kernels for 0% -> 0%
where the time goes in v1:
time: 813 us; the launch traced here: 811 us
  blocking collectives  407 us (50%)
  waiting for transfers between devices  259 us (32%)
  local copies, waits for them, and re-layouts  78.3 us (10%)
  starting transfers between devices  26.9 us (3%)
  other arithmetic  19.6 us (2%)
  matrix products  19.6 us (2%)
    all_to_all x1, blocking collectives, gather_over(): parts = lax.all_to_all(parts, mesh_axis, split_axis=0, concat_axis=0)  237 us
    all_to_all x1, waiting for transfers between devices, gather_over(): parts = lax.all_to_all(parts, mesh_axis, split_axis=0, concat_axis=0)  234 us
    all_to_all x4, blocking collectives, copy_for_each(): lax.all_to_all(jnp.broadcast_to(shard[None], (devices, *shard.shape)), ax...  90 us
    all_to_all x4, blocking collectives, summed_on_arrival(): lax.all_to_all(parts, axis, split_axis=0, concat_axis=0, tiled=True)  80.6 us
    another operation x4, local copies, waits for them, and re-layouts, block_product(): blocks = panel.reshape(count_rows, -1, block)  29.2 us
    all_to_all x1, waiting for transfers between devices, copy_for_each(): lax.all_to_all(jnp.broadcast_to(shard[None], (devices, *shard.shape)), ax...  24.9 us
  transfers between devices with their start and end apart: 2, of which 2 were waited for; matrix products, arithmetic and copies ran while one was open for 0% of the time, Pallas kernels for 0%

profile of v1, /device:TPU:1, one launch (start us, length us, event | category | flops | bytes accessed | tf_op | source)
XLA Modules:
  0.0 811.0 jit_solution(1895617640428919213)
XLA Ops:
  0.6 0.0 copy-start
  0.6 1.0 broadcast_in_dim.20
  1.7 23.5 %all_to_all.56 = f32[8,5,2048]{2,1,0:T(8,128)S(1)} all-to-all(f32[8,5,2048]{2,1,0:T(8,128)S(1)} %broadcast_in_dim.20), channel_id=1, replica_groups=mesh['row'=16,'col'=4,'cuts'=8] {'cuts'}, dimensions={0} | all-to-all | bytes 655360 | tf_op jit(solution)/shard_map/all_to_all | solution.py:16
  25.2 0.8 stack_reshape.4
  26.0 4.0 stack.6
  29.9 13.0 %all-to-all-start.1 = ((f32[16,40,2048]{2,1,0:T(8,128)}), f32[16,40,2048]{2,1,0:T(8,128)}, u32[]{:S(2)}, u32[]{:S(2)}) async-start(f32[16,40,2048]{2,1,0:T(8,128)} %stack.6), calls=%async_computation.1 | async-start | bytes 10485760 | tf_op jit(solution)/shard_map/all_to_all | solution.py:10
  43.0 233.6 %all-to-all-done.1 = f32[16,40,2048]{2,1,0:T(8,128)} async-done(((f32[16,40,2048]{2,1,0:T(8,128)}), f32[16,40,2048]{2,1,0:T(8,128)}, u32[]{:S(2)}, u32[]{:S(2)}) %all-to-all-start.1) | async-done | bytes 5242912 | tf_op jit(solution)/shard_map/all_to_all | solution.py:10
  276.6 7.9 copy.37
  284.4 6.7 reshape_reshape.12
  291.2 7.9 copy.38
  299.0 4.0 gather_fusion
  303.0 6.9 convolution_bitcast_fusion.3
  309.9 1.9 convolution_bitcast_fusion.1
  311.8 2.7 reshape_reshape.13
  314.4 2.1 copy.55
  316.5 17.4 %all_to_all.57 = f32[4,40,2048]{2,1,0:T(8,128)} all-to-all(f32[4,40,2048]{2,1,0:T(8,128)S(1)} %bitcast.48), channel_id=1, replica_groups=mesh['row'=16,'col'=4,'cuts'=8] {'col'}, dimensions={0} | all-to-all | bytes 2621440 | tf_op jit(solution)/shard_map/all_to_all | solution.py:40
  333.9 2.2 reduce_sum.56
  336.0 1.0 reshape.45
  337.1 22.8 %all_to_all.58 = f32[8,5,2048]{2,1,0:T(8,128)} all-to-all(f32[8,5,2048]{2,1,0:T(8,128)S(1)} %reshape.45), channel_id=1, replica_groups=mesh['row'=16,'col'=4,'cuts'=8] {'cuts'}, dimensions={0} | all-to-all | bytes 655360 | tf_op jit(solution)/shard_map/all_to_all | solution.py:40
  359.8 1.1 reduce_sum.57
  361.0 18.4 %all_to_all.59 = f32[8,5,2048]{2,1,0:T(8,128)} all-to-all(f32[8,5,2048]{2,1,0:T(8,128)S(1)} %broadcast_in_dim.22), channel_id=1, replica_groups=mesh['row'=16,'col'=4,'cuts'=8] {'cuts'}, dimensions={0} | all-to-all | bytes 655360 | tf_op jit(solution)/shard_map/all_to_all | solution.py:16
  379.4 1.1 reshape.46
  380.5 0.4 fusion.28
  380.9 1.1 broadcast_in_dim.23
  382.1 3.2 reshape.72
  385.2 13.9 %all-to-all-start.5 = ((f32[64,1,1600]{2,1,0:T(1,128)}), f32[64,1,1600]{2,1,0:T(1,128)}, u32[]{:S(2)}, u32[]{:S(2)}) async-start(f32[64,1,1600]{2,1,0:T(1,128)} %reshape.72), calls=%async_computation.5 | async-start | bytes 851968 | tf_op jit(solution)/shard_map/all_to_all | solution.py:16
  399.2 24.9 %all-to-all-done.5 = f32[64,1,1600]{2,1,0:T(1,128)} async-done(((f32[64,1,1600]{2,1,0:T(1,128)}), f32[64,1,1600]{2,1,0:T(1,128)}, u32[]{:S(2)}, u32[]{:S(2)}) %all-to-all-start.5) | async-done | bytes 409632 | tf_op jit(solution)/shard_map/all_to_all | solution.py:16
  424.1 0.5 broadcast.114
  424.6 3.4 reduce.6
  428.1 2.6 reshape.73
  430.7 1.4 reduce_sum.58
  432.1 0.1 copy.42
  432.2 3.6 cholesky.17
  435.9 0.6 compare_reduce_fusion
  436.5 0.7 fusion.13
  437.2 3.1 custom-call.6
  440.3 0.2 fusion.14
  440.5 0.3 fusion.20
  440.8 0.0 copy-start.1
  440.8 22.9 %all_to_all.60 = f32[8,5,2048]{2,1,0:T(8,128)} all-to-all(f32[8,5,2048]{2,1,0:T(8,128)S(1)} %broadcast_in_dim.24), channel_id=1, replica_groups=mesh['row'=16,'col'=4,'cuts'=8] {'cuts'}, dimensions={0} | all-to-all | bytes 655360 | tf_op jit(solution)/shard_map/all_to_all | solution.py:16
  463.8 1.1 stack_reshape.5
  464.9 0.6 stack.7
  465.5 236.7 %all_to_all.61 = f32[16,40,2048]{2,1,0:T(8,128)S(1)} all-to-all(f32[16,40,2048]{2,1,0:T(8,128)S(1)} %stack.7), channel_id=1, replica_groups=mesh['row'=16,'col'=4,'cuts'=8] {'row'}, dimensions={0} | all-to-all | bytes 10485760 | tf_op jit(solution)/shard_map/all_to_all | solution.py:10
  702.2 5.4 copy.43
  707.6 6.7 reshape_reshape.14
  714.3 7.9 copy.44
  722.2 4.0 gather_fusion.1
  726.2 6.9 convolution_bitcast_fusion.2
  733.1 1.9 convolution_bitcast_fusion
  734.9 2.7 reshape_reshape.15
  737.6 2.1 copy.54
  739.7 18.7 %all_to_all.62 = f32[4,40,2048]{2,1,0:T(8,128)} all-to-all(f32[4,40,2048]{2,1,0:T(8,128)S(1)} %bitcast.49), channel_id=1, replica_groups=mesh['row'=16,'col'=4,'cuts'=8] {'col'}, dimensions={0} | all-to-all | bytes 2621440 | tf_op jit(solution)/shard_map/all_to_all | solution.py:40
  758.4 1.4 reduce_sum.60
  759.8 0.8 reshape.48
  760.6 21.7 %all_to_all.63 = f32[8,5,2048]{2,1,0:T(8,128)} all-to-all(f32[8,5,2048]{2,1,0:T(8,128)} %reshape.48), channel_id=1, replica_groups=mesh['row'=16,'col'=4,'cuts'=8] {'cuts'}, dimensions={0} | all-to-all | bytes 655360 | tf_op jit(solution)/shard_map/all_to_all | solution.py:40
  782.4 1.1 reduce_sum.61
  783.4 0.3 fusion.29
  783.8 0.1 broadcast_bitcast_fusion
  783.8 0.2 reshape.74
  784.0 25.1 %all_to_all.64 = f32[64,1,200]{2,1,0:T(1,128)S(1)} all-to-all(f32[64,1,200]{2,1,0:T(1,128)S(1)} %reshape.74), channel_id=1, replica_groups=mesh['row'=16,'col'=4,'cuts'=8] {'row','col'}, dimensions={0} | all-to-all | bytes 102400 | tf_op jit(solution)/shard_map/all_to_all | solution.py:16
  809.1 0.8 reduce.7
  809.9 0.1 reshape.75
  810.0 0.1 bitcast_reduce_fusion
  810.1 0.9 convolution_subtract_fusion
  (13 shorter events, 0.2 us)
Async XLA Ops:
  0.6 302.4 %copy-start = (f32[43,128,128]{2,1,0:T(8,128)S(1)}, f32[43,128,128]{2,1,0:T(8,128)}, u32[]{:S(2)}) copy-start(f32[43,128,128]{2,1,0:T(8,128)} %param.7) | copy-start | bytes 8454148
  29.9 13.0 %copy-start.2 = (s32[43]{0:T(128)S(1)}, s32[43]{0:T(128)}, u32[]{:S(2)}) copy-start(s32[43]{0:T(128)} %param.9) | copy-start | bytes 520
  29.9 13.0 %copy-start.3 = (s32[43]{0:T(128)S(1)}, s32[43]{0:T(128)}, u32[]{:S(2)}) copy-start(s32[43]{0:T(128)} %param.8) | copy-start | bytes 520
  29.9 246.6 %all-to-all-start.1 = ((f32[16,40,2048]{2,1,0:T(8,128)}), f32[16,40,2048]{2,1,0:T(8,128)}, u32[]{:S(2)}, u32[]{:S(2)}) async-start(f32[16,40,2048]{2,1,0:T(8,128)} %stack.6), calls=%async_computation.1 | async-start | bytes 10485760 | tf_op jit(solution)/shard_map/all_to_all | solution.py:10
  385.2 38.9 %all-to-all-start.5 = ((f32[64,1,1600]{2,1,0:T(1,128)}), f32[64,1,1600]{2,1,0:T(1,128)}, u32[]{:S(2)}, u32[]{:S(2)}) async-start(f32[64,1,1600]{2,1,0:T(1,128)} %reshape.72), calls=%async_computation.5 | async-start | bytes 851968 | tf_op jit(solution)/shard_map/all_to_all | solution.py:16
  440.8 24.7 %copy-start.1 = (f32[5,2048]{1,0:T(8,128)}, f32[5,2048]{1,0:T(8,128)S(1)}, u32[]{:S(2)}) copy-start(f32[5,2048]{1,0:T(8,128)S(1)} %fusion.20) | copy-start | bytes 122884
